TPU v7x, 32 devices: a whole 2x2x4 slice. The times are simulated.
32 devices in a mesh: rows: 4 (over y, x), batch: 8 (over z, core).
Axes of the slice: x: 2, y: 2, z: 4, core: 2. Of those that a mesh axis runs over, the one named last changes fastest.
Arguments:
- control: bfloat16 [8, 24, 96, 320], P('batch', 'rows'), may hold values from -60 to 60, as said below
- unet_skips: bfloat16 [2, 8, 24, 96, 320], P(None, 'batch', 'rows'), may hold values from -6 to 6
- norm_gains: float32 [2, 2, 320], replicated, may hold values from 0.25 to 1.75
- norm_shifts: float32 [2, 2, 320], replicated, may hold values from -3 to 3
- conv_weights: bfloat16 [2, 2, 3, 960, 320], P(None, None, None, None, 'batch'), may hold values from -0.109375 to 0.109375
- zero_weights: bfloat16 [2, 1, 320, 320], P(None, None, None, 'batch'), may hold values from -0.3125 to 0.3125
Outputs:
- controls: bfloat16 [2, 8, 24, 96, 320], P(None, 'batch', 'rows')
Inputs may be any that keep to these rules, and one draw needn't show every extreme that they name: `control`: Real-valued latent features.
All inputs are finite; a program needn't handle non-finite values.
Results may differ from a plain program's by a relative error of at most 0.01.
Values may be sent and summed in bfloat16 or wider, within the bound.
A program may use at most 64 MiB of HBM per device.

v0:
```python
import jax
import jax.numpy as jnp
from jax import lax
from jax.sharding import PartitionSpec as P

GROUPS = 32
epsilon = 1e-05


def extended(block, sides, width):
    for axis, dim in sides:
        count = lax.axis_size(axis)
        forward = [(i, i + 1) for i in range(count - 1)]
        backward = [(target, source) for source, target in forward]
        low = lax.ppermute(
            lax.slice_in_dim(block, block.shape[dim] - width, None, axis=dim), axis, forward
        )
        high = lax.ppermute(lax.slice_in_dim(block, 0, width, axis=dim), axis, backward)
        block = jnp.concatenate([low, block, high], axis=dim)
    return block


def normalize(values, gain_row, shift_row):
    samples, height, across, channels = values.shape
    members = height * lax.axis_size("rows") * across * (channels // GROUPS)
    grouped = values.astype(jnp.float32).reshape(
        samples, height, across, GROUPS, channels // GROUPS
    )
    partial_sum, partial_square = lax.psum(
        (
            jnp.sum(grouped, axis=(1, 2, 4), keepdims=True),
            jnp.sum(grouped * grouped, axis=(1, 2, 4), keepdims=True),
        ),
        "rows",
    )
    average = partial_sum / members
    spread = partial_square / members - average * average
    centered = grouped - average
    scaled = (centered * lax.rsqrt(spread + epsilon)).reshape(
        samples, height, across, channels
    ) * gain_row + shift_row
    return jax.nn.silu(scaled).astype(jnp.bfloat16)


def apply_taps(padded, weight_piece):
    tap_rows = weight_piece.shape[0]
    tap_cols = weight_piece.shape[1] // padded.shape[3]
    height = padded.shape[1] - tap_rows + 1
    across = padded.shape[2] - tap_cols + 1
    summed = jnp.zeros((padded.shape[0], height, across, weight_piece.shape[2]), jnp.float32)
    for row_tap in range(tap_rows):
        row_band = padded[:, row_tap : row_tap + height]
        if tap_cols > 1:
            stacked = jnp.concatenate(
                [row_band[:, :, col_tap : col_tap + across] for col_tap in range(tap_cols)], axis=3
            )
        else:
            stacked = row_band
        summed = summed + jnp.einsum(
            "bhwk,kc->bhwc", stacked, weight_piece[row_tap], preferred_element_type=jnp.float32
        )
    return summed


def convolve(values, weight):
    if weight.shape[0] > 1:
        padded = extended(values, (("rows", 1),), 1)
        padded = jnp.pad(padded, ((0, 0), (0, 0), (1, 1), (0, 0)))
    else:
        padded = values
    complete = lax.all_gather(weight, "batch", axis=2, tiled=True)
    return apply_taps(padded, complete)


def on_device(control, unet_skips, norm_gains, norm_shifts, conv_weights, zero_weights):
    hidden = control
    results = []
    for layer_index in range(conv_weights.shape[0]):
        normed = normalize(hidden, norm_gains[layer_index, 0], norm_shifts[layer_index, 0])
        first = convolve(normed, conv_weights[layer_index, 0]).astype(jnp.bfloat16)
        normed_two = normalize(first, norm_gains[layer_index, 1], norm_shifts[layer_index, 1])
        second = convolve(normed_two, conv_weights[layer_index, 1])
        hidden = (hidden.astype(jnp.float32) + second).astype(jnp.bfloat16)
        zeroed = convolve(hidden, zero_weights[layer_index])
        results.append((zeroed + unet_skips[layer_index].astype(jnp.float32)).astype(jnp.bfloat16))
    return jnp.stack(results)


def solution(mesh):
    placed = (
        P("batch", "rows", None, None),
        P(None, "batch", "rows", None, None),
        P(),
        P(),
        P(None, None, None, None, "batch"),
        P(None, None, None, "batch"),
    )
    return jax.shard_map(
        on_device,
        mesh=mesh,
        in_specs=placed,
        out_specs=P(None, "batch", "rows", None, None),
        check_vma=False,
    )
```

profile of v0, /device:TPU:0, one launch (start us, length us, event | category | flops | bytes accessed | tf_op | source)
XLA Modules:
  0.0 152.8 jit_solution(14512298526885135947)
XLA Ops:
  6.6 2.3 %fusion.153 = (bf16[1,1,3,960,40]{3,4,2,1,0:T(8,128)(2,1)}, bf16[1,1,3,960,40]{3,4,2,1,0:T(8,128)(2,1)}, bf16[1,1,3,960,40]{3,4,2,1,0:T(8,128)(2,1)}, bf16[1,1,3,960,40]{3,4,2,1,0:T(8,128)(2,1)}) fusion(bf16[2,2,3,960,40]{3,4,2,1,0:T(8,128)(2,1)} %param.10), kind=kLoop, calls=%fused_computation.215 | loop fusion | bytes 1843200 | tf_op jit(solution)/shard_map/slice | solution.py:82
  9.0 0.7 all-gather.13.cloned.1.call-update
  9.7 0.7 all-gather.15.cloned.1.call-update
  10.5 0.2 convert_reduce_fusion.1
  10.8 0.1 reduce_sum.97
  10.9 0.1 reduce_sum.100
  11.1 11.4 %all-reduce.7 = (f32[1,1,1,32,1]{3,4,2,1,0:T(1,128)S(1)}, f32[1,1,1,32,1]{3,4,2,1,0:T(1,128)S(1)}) all-reduce(f32[1,1,1,32,1]{3,4,2,1,0:T(1,128)S(1)} %bitcast.189, f32[1,1,1,32,1]{3,4,2,1,0:T(1,128)S(1)} %bitcast.187), channel_id=1, replica_groups=mesh['rows'=4,'batch'=8] {'rows'}, use_global_device_ids=true, to_apply=%region_5.6 | all-reduce | flops 64 | bytes 512 | tf_op jit(solution)/shard_map/psum | solution.py:29
  22.5 0.1 mul.189
  22.9 0.6 slice_reduce_fusion
  23.5 0.3 fusion.116
  23.8 2.2 %collective-permute-start = (bf16[1,1,96,320]{3,2,1,0:T(8,128)(2,1)S(1)}, bf16[1,1,96,320]{3,2,1,0:T(8,128)(2,1)}, u32[]{:S(2)}, u32[]{:S(2)}) collective-permute-start(bf16[1,1,96,320]{3,2,1,0:T(8,128)(2,1)S(1)} %get-tuple-element.64), channel_id=1, source_target_pairs={{0,8},{8,16},{16,24},{1,9},{9,17},{17,25},{2,10},{10,18},{18,26},{... | collective-permute-start | bytes 184328 | tf_op jit(solution)/shard_map/ppermute | solution.py:15
  26.0 1.3 collective-permute-start.1
  27.3 0.6 fusion.162
  28.0 4.3 %collective-permute-done.1 = bf16[1,1,96,320]{3,2,1,0:T(8,128)(2,1)S(1)} collective-permute-done((bf16[1,1,96,320]{3,2,1,0:T(8,128)(2,1)S(1)}, bf16[1,1,96,320]{3,2,1,0:T(8,128)(2,1)S(1)}, u32[]{:S(2)}, u32[]{:S(2)}) %collective-permute-start.1) | collective-permute-done | bytes 61472 | tf_op jit(solution)/shard_map/ppermute | solution.py:18
  32.2 0.6 copy-done.5
  32.9 1.1 fusion.134
  33.9 0.3 fusion.157
  34.3 5.6 %all-gather.11.cloned.1.call-done = bf16[1,1,3,960,320]{3,4,2,1,0:T(8,128)(2,1)} async-done(((bf16[1,1,3,960,40]{3,4,2,1,0:T(8,128)(2,1)}), bf16[1,1,3,960,320]{3,4,2,1,0:T(8,128)(2,1)}) %all-gather.11.cloned.1.call-update) | async-done | bytes 1843216 | tf_op jit(solution)/shard_map/all_gather | solution.py:71
  39.9 2.0 %fusion.53 = f32[6,96,320]{2,1,0:T(8,128)S(1)} fusion(bf16[1,6,96,320]{3,2,1,0:T(8,128)(2,1)S(1)} %fusion.116, bf16[1,1,96,320]{3,2,1,0:T(8,128)(2,1)} %collective-permute-done, bf16[1,6,96,320]{3,2,1,0:T(8,128)(2,1)S(1)} %get-tuple-element.54, bf16[1,6,96,320]{3,2,1,0:T(8,128)(2,1)S(1)} %get-tuple-element.55, ...), kind=kOutput, calls=%fused_computation.80 | convolution fusion | flops 358318080 | bytes 2572288 | tf_op jit(solution)/shard_map/bhwk,kc->bhwc/dot_general | solution.py:59
  41.9 0.8 convolution_add_fusion.9
  42.8 0.8 convert_reduce_fusion.3
  43.8 0.1 reduce_sum.106
  44.0 0.1 reduce_sum.112
  44.1 9.8 %all-reduce.6 = (f32[1,1,1,32,1]{3,4,2,1,0:T(1,128)S(1)}, f32[1,1,1,32,1]{3,4,2,1,0:T(1,128)S(1)}) all-reduce(f32[1,1,1,32,1]{3,4,2,1,0:T(1,128)S(1)} %bitcast.190, f32[1,1,1,32,1]{3,4,2,1,0:T(1,128)S(1)} %bitcast.185), channel_id=1, replica_groups=mesh['rows'=4,'batch'=8] {'rows'}, use_global_device_ids=true, to_apply=%region_11.12 | all-reduce | flops 64 | bytes 512 | tf_op jit(solution)/shard_map/psum | solution.py:29
  54.0 0.1 mul.200
  54.3 0.3 fusion.136
  54.7 1.7 %collective-permute-start.2 = (bf16[1,1,96,320]{3,2,1,0:T(8,128)(2,1)S(1)}, bf16[1,1,96,320]{3,2,1,0:T(8,128)(2,1)S(1)}, u32[]{:S(2)}, u32[]{:S(2)}) collective-permute-start(bf16[1,1,96,320]{3,2,1,0:T(8,128)(2,1)S(1)} %get-tuple-element.62), channel_id=1, source_target_pairs={{0,8},{8,16},{16,24},{1,9},{9,17},{17,25},{2,10},{10,18},{18,26},{... | collective-permute-start | bytes 184328 | tf_op jit(solution)/shard_map/ppermute | solution.py:15
  56.4 1.3 collective-permute-start.3
  57.7 16.0 %all-gather.5 = bf16[1,1,320,320]{2,3,1,0:T(8,128)(2,1)} all-gather(bf16[1,1,320,40]{2,3,1,0:T(8,128)(2,1)S(1)} %copy-done.4), channel_id=7, replica_groups=mesh['rows'=4,'batch'=8] {'batch'}, dimensions={3}, use_global_device_ids=true | all-gather | bytes 230400 | tf_op jit(solution)/shard_map/all_gather | solution.py:71
  73.7 0.6 copy-done.11
  74.3 0.6 copy-done.7
  74.9 0.2 select_maximum_fusion.4
  75.1 0.3 fusion.156
  75.5 2.1 %fusion.42 = f32[6,96,320]{2,1,0:T(8,128)S(1)} fusion(bf16[1,6,96,320]{3,2,1,0:T(8,128)(2,1)S(1)} %fusion.136, bf16[1,1,96,320]{3,2,1,0:T(8,128)(2,1)} %copy-done.11, bf16[1,6,96,320]{3,2,1,0:T(8,128)(2,1)S(1)} %get-tuple-element.48, bf16[1,6,96,320]{3,2,1,0:T(8,128)(2,1)S(1)} %get-tuple-element.49, ...), kind=kOutput, calls=%fused_computation.69 | convolution fusion | flops 358318080 | bytes 2572288 | tf_op jit(solution)/shard_map/bhwk,kc->bhwc/dot_general | solution.py:59
  77.5 0.8 convolution_add_fusion.7
  78.4 0.9 convert_reduce_fusion
  79.4 0.1 reduce_sum.115
  79.6 0.1 reduce_sum.145
  79.7 11.0 %all-reduce.5 = (f32[1,1,1,32,1]{3,4,2,1,0:T(1,128)S(1)}, f32[1,1,1,32,1]{3,4,2,1,0:T(1,128)S(1)}) all-reduce(f32[1,1,1,32,1]{3,4,2,1,0:T(1,128)S(1)} %bitcast.191, f32[1,1,1,32,1]{3,4,2,1,0:T(1,128)S(1)} %bitcast.186), channel_id=1, replica_groups=mesh['rows'=4,'batch'=8] {'rows'}, use_global_device_ids=true, to_apply=%region_17.18 | all-reduce | flops 64 | bytes 512 | tf_op jit(solution)/shard_map/psum | solution.py:29
  91.1 0.3 fusion.126
  91.4 3.3 %collective-permute-start.4 = (bf16[1,1,96,320]{3,2,1,0:T(8,128)(2,1)S(1)}, bf16[1,1,96,320]{3,2,1,0:T(8,128)(2,1)S(1)}, u32[]{:S(2)}, u32[]{:S(2)}) collective-permute-start(bf16[1,1,96,320]{3,2,1,0:T(8,128)(2,1)S(1)} %get-tuple-element.60), channel_id=1, source_target_pairs={{0,8},{8,16},{16,24},{1,9},{9,17},{17,25},{2,10},{10,18},{18,26},{... | collective-permute-start | bytes 184328 | tf_op jit(solution)/shard_map/ppermute | solution.py:15
  94.8 1.3 collective-permute-start.5
  96.1 14.3 %all-gather.2 = bf16[1,1,320,320]{2,3,1,0:T(8,128)(2,1)S(1)} all-gather(bf16[1,1,320,40]{2,3,1,0:T(8,128)(2,1)S(1)} %copy-done.3), channel_id=4, replica_groups=mesh['rows'=4,'batch'=8] {'batch'}, dimensions={3}, use_global_device_ids=true | all-gather | bytes 230400 | tf_op jit(solution)/shard_map/all_gather | solution.py:71
  110.4 0.2 select_maximum_fusion.2
  110.6 1.0 fusion.155
  111.6 2.2 %fusion.31 = f32[6,96,320]{2,1,0:T(8,128)S(1)} fusion(bf16[1,6,96,320]{3,2,1,0:T(8,128)(2,1)S(1)} %fusion.126, bf16[1,1,96,320]{3,2,1,0:T(8,128)(2,1)S(1)} %collective-permute-done.4, bf16[1,6,96,320]{3,2,1,0:T(8,128)(2,1)S(1)} %get-tuple-element.42, bf16[1,6,96,320]{3,2,1,0:T(8,128)(2,1)} %get-tuple-element.43, ...), kind=kOutput, calls=%fused_computation.58 | convolution fusion | flops 358318080 | bytes 2633728 | tf_op jit(solution)/shard_map/bhwk,kc->bhwc/dot_general | solution.py:59
  113.8 0.8 convolution_add_fusion.5
  114.7 0.8 convert_reduce_fusion.2
  115.6 0.1 reduce_sum.148
  115.8 0.1 reduce_sum.151
  115.9 11.1 %all-reduce.4 = (f32[1,1,1,32,1]{3,4,2,1,0:T(1,128)S(1)}, f32[1,1,1,32,1]{3,4,2,1,0:T(1,128)S(1)}) all-reduce(f32[1,1,1,32,1]{3,4,2,1,0:T(1,128)S(1)} %bitcast.188, f32[1,1,1,32,1]{3,4,2,1,0:T(1,128)S(1)} %bitcast.184), channel_id=1, replica_groups=mesh['rows'=4,'batch'=8] {'rows'}, use_global_device_ids=true, to_apply=%region_23.24 | all-reduce | flops 64 | bytes 512 | tf_op jit(solution)/shard_map/psum | solution.py:29
  127.4 0.3 fusion.135
  127.7 1.9 %collective-permute-start.6 = (bf16[1,1,96,320]{3,2,1,0:T(8,128)(2,1)S(1)}, bf16[1,1,96,320]{3,2,1,0:T(8,128)(2,1)S(1)}, u32[]{:S(2)}, u32[]{:S(2)}) collective-permute-start(bf16[1,1,96,320]{3,2,1,0:T(8,128)(2,1)S(1)} %get-tuple-element.58), channel_id=1, source_target_pairs={{0,8},{8,16},{16,24},{1,9},{9,17},{17,25},{2,10},{10,18},{18,26},{... | collective-permute-start | bytes 184328 | tf_op jit(solution)/shard_map/ppermute | solution.py:15
  129.6 1.3 collective-permute-start.7
  130.9 0.4 fusion.10
  131.4 0.2 collective-permute-done.6
  131.6 4.3 %collective-permute-done.7 = bf16[1,1,96,320]{3,2,1,0:T(8,128)(2,1)S(1)} collective-permute-done((bf16[1,1,96,320]{3,2,1,0:T(8,128)(2,1)S(1)}, bf16[1,1,96,320]{3,2,1,0:T(8,128)(2,1)S(1)}, u32[]{:S(2)}, u32[]{:S(2)}) %collective-permute-start.7) | collective-permute-done | bytes 61472 | tf_op jit(solution)/shard_map/ppermute | solution.py:18
  135.9 0.6 copy-done.9
  136.5 0.2 select_maximum_fusion
  136.7 1.0 fusion.154
  137.7 2.0 %fusion.20 = f32[6,96,320]{2,1,0:T(8,128)S(1)} fusion(bf16[1,6,96,320]{3,2,1,0:T(8,128)(2,1)S(1)} %fusion.135, bf16[1,1,96,320]{3,2,1,0:T(8,128)(2,1)} %copy-done.12, bf16[1,6,96,320]{3,2,1,0:T(8,128)(2,1)S(1)} %get-tuple-element.36, bf16[1,6,96,320]{3,2,1,0:T(8,128)(2,1)} %get-tuple-element.37, bf16[1,1,3,960,320]{3,4,2,1,0:T(8,128)(2,1)} %all-gather.17.cloned.1.call-done), kind=kOutput, calls=%fused_computation.47 | convolution fusion | flops 358318080 | bytes 2646016 | tf_op jit(solution)/shard_map/bhwk,kc->bhwc/dot_general | solution.py:59
  139.8 2.8 %convolution_add_fusion.3 = f32[6,96,320]{2,1,0:T(8,128)} fusion(f32[6,96,320]{2,1,0:T(8,128)S(1)} %fusion.20, bf16[1,6,96,320]{3,2,1,0:T(8,128)(2,1)S(1)} %get-tuple-element.34, bf16[1,6,96,320]{3,2,1,0:T(8,128)(2,1)S(1)} %fusion.135, bf16[1,6,96,320]{3,2,1,0:T(8,128)(2,1)S(1)} %get-tuple-element.35, ...), kind=kOutput, calls=%fused_computation.20 | convolution fusion | flops 357396480 | bytes 3235840 | tf_op jit(solution)/shard_map/bhwk,kc->bhwc/dot_general | solution.py:59
  142.7 2.5 %fusion.9 = bf16[1,1,6,96,320]{4,3,2,1,0:T(8,128)(2,1)S(1)} fusion(f32[6,96,320]{2,1,0:T(8,128)} %convolution_add_fusion.3, bf16[1,6,96,320]{3,2,1,0:T(8,128)(2,1)S(1)} %get-tuple-element.76, bf16[1,1,96,320]{3,2,1,0:T(8,128)(2,1)S(1)} %copy-done.10, bf16[1,6,96,320]{3,2,1,0:T(8,128)(2,1)S(1)} %fusion.135, ...), kind=kOutput, calls=%fused_computation.35 | convolution fusion | flops 477573120 | bytes 4091904 | tf_op jit(solution)/shard_map/bhwk,kc->bhwc/dot_general | solution.py:59
  145.2 1.1 pad_maximum_fusion.8
  (82 shorter events, 2.6 us)
Async XLA Ops:
  6.5 3.9 %copy-start = (bf16[1,6,96,320]{3,2,1,0:T(8,128)(2,1)S(1)}, bf16[1,6,96,320]{3,2,1,0:T(8,128)(2,1)}, u32[]{:S(2)}) copy-start(bf16[1,6,96,320]{3,2,1,0:T(8,128)(2,1)} %param.6) | copy-start | bytes 1105924
  6.5 16.3 %copy-start.17 = (f32[2,2,320]{2,1,0:T(2,128)S(1)}, f32[2,2,320]{2,1,0:T(2,128)}, u32[]{:S(2)}) copy-start(f32[2,2,320]{2,1,0:T(2,128)} %param.8) | copy-start | bytes 15364
  6.5 16.3 %copy-start.16 = (f32[2,2,320]{2,1,0:T(2,128)S(1)}, f32[2,2,320]{2,1,0:T(2,128)}, u32[]{:S(2)}) copy-start(f32[2,2,320]{2,1,0:T(2,128)} %param.9) | copy-start | bytes 15364
  6.5 20.8 %copy-start.13 = (bf16[2,1,320,40]{2,3,1,0:T(8,128)(2,1)S(1)}, bf16[2,1,320,40]{2,3,1,0:T(8,128)(2,1)}, u32[]{:S(2)}) copy-start(bf16[2,1,320,40]{2,3,1,0:T(8,128)(2,1)} %param.11) | copy-start | bytes 153604
  6.5 33.3 %all-gather.11.cloned.1.call-start = ((), (), s32[]{:S(2)}) async-start(), calls=%async_computation | async-start | bytes 2211840 | tf_op jit(solution)/shard_map/all_gather | solution.py:71
  8.9 66.5 %all-gather.13.cloned.1.call-start = ((), (), s32[]{:S(2)}) async-start(), calls=%async_computation.1 | async-start | bytes 2211840 | tf_op jit(solution)/shard_map/all_gather | solution.py:71
  9.7 102.0 %all-gather.15.cloned.1.call-start = ((), (), s32[]{:S(2)}) async-start(), calls=%async_computation.2 | async-start | bytes 2211840 | tf_op jit(solution)/shard_map/all_gather | solution.py:71
  10.4 127.3 %all-gather.17.cloned.1.call-start = ((), (), s32[]{:S(2)}) async-start(), calls=%async_computation.3 | async-start | bytes 2211840 | tf_op jit(solution)/shard_map/all_gather | solution.py:71
  23.8 4.1 %collective-permute-start = (bf16[1,1,96,320]{3,2,1,0:T(8,128)(2,1)S(1)}, bf16[1,1,96,320]{3,2,1,0:T(8,128)(2,1)}, u32[]{:S(2)}, u32[]{:S(2)}) collective-permute-start(bf16[1,1,96,320]{3,2,1,0:T(8,128)(2,1)S(1)} %get-tuple-element.64), channel_id=1, source_target_pairs={{0,8},{8,16},{16,24},{1,9},{9,17},{17,25},{2,10},{10,18},{18,26},{... | collective-permute-start | bytes 184328 | tf_op jit(solution)/shard_map/ppermute | solution.py:15
  26.0 6.2 %collective-permute-start.1 = (bf16[1,1,96,320]{3,2,1,0:T(8,128)(2,1)S(1)}, bf16[1,1,96,320]{3,2,1,0:T(8,128)(2,1)S(1)}, u32[]{:S(2)}, u32[]{:S(2)}) collective-permute-start(bf16[1,1,96,320]{3,2,1,0:T(8,128)(2,1)S(1)} %get-tuple-element.63), channel_id=1, source_target_pairs={{8,0},{16,8},{24,16},{9,1},{17,9},{25,17},{10,2},{18,10},{26,18},{... | collective-permute-start | bytes 184328 | tf_op jit(solution)/shard_map/ppermute | solution.py:18
  32.2 0.6 copy-start.5
  39.9 2.1 %copy-start.20 = (bf16[1,1,3,960,320]{3,4,2,1,0:T(8,128)(2,1)S(1)}, bf16[1,1,3,960,320]{3,4,2,1,0:T(8,128)(2,1)}, u32[]{:S(2)}) copy-start(bf16[1,1,3,960,320]{3,4,2,1,0:T(8,128)(2,1)} %all-gather.11.cloned.1.call-done) | copy-start | bytes 5529604
  41.9 0.9 copy-start.6
  42.8 11.5 %copy-start.14 = (f32[320]{0:T(512)S(1)}, f32[320]{0:T(512)}, u32[]{:S(2)}) copy-start(f32[320]{0:T(512)} %get-tuple-element.18) | copy-start | bytes 3844
  42.8 11.5 %copy-start.15 = (f32[320]{0:T(512)S(1)}, f32[320]{0:T(512)}, u32[]{:S(2)}) copy-start(f32[320]{0:T(512)} %get-tuple-element.80) | copy-start | bytes 3844
  42.8 14.9 %copy-start.4 = (bf16[1,1,320,40]{2,3,1,0:T(8,128)(2,1)S(1)}, bf16[1,1,320,40]{2,3,1,0:T(8,128)(2,1)}, u32[]{:S(2)}) copy-start(bf16[1,1,320,40]{2,3,1,0:T(8,128)(2,1)} %get-tuple-element.66) | copy-start | bytes 76804
  54.7 19.0 %collective-permute-start.2 = (bf16[1,1,96,320]{3,2,1,0:T(8,128)(2,1)S(1)}, bf16[1,1,96,320]{3,2,1,0:T(8,128)(2,1)S(1)}, u32[]{:S(2)}, u32[]{:S(2)}) collective-permute-start(bf16[1,1,96,320]{3,2,1,0:T(8,128)(2,1)S(1)} %get-tuple-element.62), channel_id=1, source_target_pairs={{0,8},{8,16},{16,24},{1,9},{9,17},{17,25},{2,10},{10,18},{18,26},{... | collective-permute-start | bytes 184328 | tf_op jit(solution)/shard_map/ppermute | solution.py:15
  56.4 17.3 %collective-permute-start.3 = (bf16[1,1,96,320]{3,2,1,0:T(8,128)(2,1)S(1)}, bf16[1,1,96,320]{3,2,1,0:T(8,128)(2,1)S(1)}, u32[]{:S(2)}, u32[]{:S(2)}) collective-permute-start(bf16[1,1,96,320]{3,2,1,0:T(8,128)(2,1)S(1)} %get-tuple-element.61), channel_id=1, source_target_pairs={{8,0},{16,8},{24,16},{9,1},{17,9},{25,17},{10,2},{18,10},{26,18},{... | collective-permute-start | bytes 184328 | tf_op jit(solution)/shard_map/ppermute | solution.py:18
  73.7 0.6 copy-start.11
  74.3 0.6 copy-start.7
  75.4 2.1 %copy-start.19 = (bf16[1,1,3,960,320]{3,4,2,1,0:T(8,128)(2,1)S(1)}, bf16[1,1,3,960,320]{3,4,2,1,0:T(8,128)(2,1)}, u32[]{:S(2)}) copy-start(bf16[1,1,3,960,320]{3,4,2,1,0:T(8,128)(2,1)} %all-gather.13.cloned.1.call-done) | copy-start | bytes 5529604
  77.5 0.9 copy-start.8
  78.4 17.7 %copy-start.3 = (bf16[1,1,320,40]{2,3,1,0:T(8,128)(2,1)S(1)}, bf16[1,1,320,40]{2,3,1,0:T(8,128)(2,1)}, u32[]{:S(2)}) copy-start(bf16[1,1,320,40]{2,3,1,0:T(8,128)(2,1)} %get-tuple-element.65) | copy-start | bytes 76804
  91.4 19.0 %collective-permute-start.4 = (bf16[1,1,96,320]{3,2,1,0:T(8,128)(2,1)S(1)}, bf16[1,1,96,320]{3,2,1,0:T(8,128)(2,1)S(1)}, u32[]{:S(2)}, u32[]{:S(2)}) collective-permute-start(bf16[1,1,96,320]{3,2,1,0:T(8,128)(2,1)S(1)} %get-tuple-element.60), channel_id=1, source_target_pairs={{0,8},{8,16},{16,24},{1,9},{9,17},{17,25},{2,10},{10,18},{18,26},{... | collective-permute-start | bytes 184328 | tf_op jit(solution)/shard_map/ppermute | solution.py:15
  94.8 15.7 %collective-permute-start.5 = (bf16[1,1,96,320]{3,2,1,0:T(8,128)(2,1)S(1)}, bf16[1,1,96,320]{3,2,1,0:T(8,128)(2,1)S(1)}, u32[]{:S(2)}, u32[]{:S(2)}) collective-permute-start(bf16[1,1,96,320]{3,2,1,0:T(8,128)(2,1)S(1)} %get-tuple-element.59), channel_id=1, source_target_pairs={{8,0},{16,8},{24,16},{9,1},{17,9},{25,17},{10,2},{18,10},{26,18},{... | collective-permute-start | bytes 184328 | tf_op jit(solution)/shard_map/ppermute | solution.py:18
  111.6 2.2 %copy-start.18 = (bf16[1,1,3,960,320]{3,4,2,1,0:T(8,128)(2,1)S(1)}, bf16[1,1,3,960,320]{3,4,2,1,0:T(8,128)(2,1)}, u32[]{:S(2)}) copy-start(bf16[1,1,3,960,320]{3,4,2,1,0:T(8,128)(2,1)} %all-gather.15.cloned.1.call-done) | copy-start | bytes 5529604
  114.6 16.3 %copy-start.2 = (bf16[2,1,6,96,320]{4,3,2,1,0:T(8,128)(2,1)S(1)}, bf16[2,1,6,96,320]{4,3,2,1,0:T(8,128)(2,1)}, u32[]{:S(2)}) copy-start(bf16[2,1,6,96,320]{4,3,2,1,0:T(8,128)(2,1)} %param.7) | copy-start | bytes 2211844
  127.7 3.8 %collective-permute-start.6 = (bf16[1,1,96,320]{3,2,1,0:T(8,128)(2,1)S(1)}, bf16[1,1,96,320]{3,2,1,0:T(8,128)(2,1)S(1)}, u32[]{:S(2)}, u32[]{:S(2)}) collective-permute-start(bf16[1,1,96,320]{3,2,1,0:T(8,128)(2,1)S(1)} %get-tuple-element.58), channel_id=1, source_target_pairs={{0,8},{8,16},{16,24},{1,9},{9,17},{17,25},{2,10},{10,18},{18,26},{... | collective-permute-start | bytes 184328 | tf_op jit(solution)/shard_map/ppermute | solution.py:15
  129.6 6.3 %collective-permute-start.7 = (bf16[1,1,96,320]{3,2,1,0:T(8,128)(2,1)S(1)}, bf16[1,1,96,320]{3,2,1,0:T(8,128)(2,1)S(1)}, u32[]{:S(2)}, u32[]{:S(2)}) collective-permute-start(bf16[1,1,96,320]{3,2,1,0:T(8,128)(2,1)S(1)} %get-tuple-element.57), channel_id=1, source_target_pairs={{8,0},{16,8},{24,16},{9,1},{17,9},{25,17},{10,2},{18,10},{26,18},{... | collective-permute-start | bytes 184328 | tf_op jit(solution)/shard_map/ppermute | solution.py:18
  131.6 4.3 %copy-start.12 = (bf16[1,1,96,320]{3,2,1,0:T(8,128)(2,1)}, bf16[1,1,96,320]{3,2,1,0:T(8,128)(2,1)S(1)}, u32[]{:S(2)}) copy-start(bf16[1,1,96,320]{3,2,1,0:T(8,128)(2,1)S(1)} %collective-permute-done.6) | copy-start | bytes 184324
  135.9 0.6 copy-start.9
  139.8 2.9 %copy-start.1 = (bf16[1,1,320,320]{2,3,1,0:T(8,128)(2,1)S(1)}, bf16[1,1,320,320]{2,3,1,0:T(8,128)(2,1)}, u32[]{:S(2)}) copy-start(bf16[1,1,320,320]{2,3,1,0:T(8,128)(2,1)} %all-gather.5) | copy-start | bytes 614404
  139.8 2.9 %copy-start.10 = (bf16[1,1,96,320]{3,2,1,0:T(8,128)(2,1)S(1)}, bf16[1,1,96,320]{3,2,1,0:T(8,128)(2,1)}, u32[]{:S(2)}) copy-start(bf16[1,1,96,320]{3,2,1,0:T(8,128)(2,1)} %copy-done.9) | copy-start | bytes 184324
Sparse Core Ops, SparseCore 0:
  9.0 30.7 all-gather.10
  41.5 29.1 all-gather.12
  72.2 27.3 all-gather.14
  101.1 27.4 all-gather.16
where the time goes:
time: 154 us; the launch traced here: 153 us
  blocking collectives  73.5 us (48%)
  matrix products  19.1 us (12%)
  waiting for transfers between devices  15.9 us (10%)
  starting transfers between devices  14.4 us (9%)
  between operations  13.6 us (9%)
  local copies, waits for them, and re-layouts  11.2 us (7%)
  other arithmetic  5.14 us (3%)
    psum x4, blocking collectives, normalize(): lax.psum((jnp.sum(grouped, axis=(1, 2, 4), keepdims=True), jnp.sum(groupe...  43.2 us
    all_gather x2, blocking collectives, convolve(): complete = lax.all_gather(weight, 'batch', axis=2, tiled=True)  30.3 us
    dot_general x13, matrix products, apply_taps(): jnp.einsum('bhwk,kc->bhwc', stacked, weight_piece[row_tap], preferred_ele...  19.1 us
    ppermute x4, starting transfers between devices, extended(): lax.ppermute(lax.slice_in_dim(block, block.shape[dim] - width, None, axis...  9.07 us
    ppermute x4, waiting for transfers between devices, extended(): lax.ppermute(lax.slice_in_dim(block, 0, width, axis=dim), axis, backward)  8.61 us
    all_gather x4, waiting for transfers between devices, convolve(): complete = lax.all_gather(weight, 'batch', axis=2, tiled=True)  5.62 us
    ppermute x4, starting transfers between devices, extended(): lax.ppermute(lax.slice_in_dim(block, 0, width, axis=dim), axis, backward)  5.16 us
  transfers between devices with their start and end apart: 12, of which 4 were waited for; matrix products, arithmetic and copies ran while one was open for 14% of the time, Pallas kernels for 0%

commit v1 on v0

--- a/solution.py
+++ b/solution.py
@@ -68,7 +68,7 @@
         padded = jnp.pad(padded, ((0, 0), (0, 0), (1, 1), (0, 0)))
     else:
         padded = values
-    complete = lax.all_gather(weight, "batch", axis=2, tiled=True)
+    complete = jnp.concatenate(lax.all_gather(weight, "batch"), axis=2)
     return apply_taps(padded, complete)
 
 

time: 154 us -> 172 us (1.12)
  waiting for transfers between devices: 15.9 us -> 28.3 us
  local copies, waits for them, and re-layouts: 11.2 us -> 23.5 us
  matrix products: 19.1 us -> 14.4 us
    all_gather x4, waiting for transfers between devices: 5.62 us -> 23.1 us  [convolve(): complete = jnp.concatenate(lax.all_gather(weight, 'batch'), axis=2)]
    slice x1 -> x5, local copies, waits for them, and re-layouts: 2.3 us -> 12.3 us  [the longest x4 9.91 us: apply_taps(): weight_piece[row_tap]]
    ppermute x4, waiting for transfers between devices: 8.61 us -> 3.84 us  [extended(): lax.ppermute(lax.slice_in_dim(block, 0, width, axis=dim), axis, backward)]
    dot_general x13, matrix products: 19.1 us -> 14.4 us  [apply_taps(): jnp.einsum('bhwk,kc->bhwc', stacked, weight_piece[row_tap], preferred_ele...]
    unnamed x42 -> x38, local copies, waits for them, and re-layouts: 2.68 us -> 4.7 us
  transfers between devices with their start and end apart: 12 -> 12, of which waited for: 4 -> 3; matrix products, arithmetic and copies ran while one was open for 14% -> 14% of each run, Pallas kernels for 0% -> 0%
where the time goes in v1:
time: 172 us; the launch traced here: 171 us
  blocking collectives  73.6 us (43%)
  waiting for transfers between devices  28.3 us (16%)
  local copies, waits for them, and re-layouts  23.5 us (14%)
  matrix products  14.4 us (8%)
  between operations  13.6 us (8%)
  starting transfers between devices  13.4 us (8%)
  other arithmetic  4.24 us (2%)
    psum x4, blocking collectives, normalize(): lax.psum((jnp.sum(grouped, axis=(1, 2, 4), keepdims=True), jnp.sum(groupe...  42.2 us
    all_gather x2, blocking collectives, convolve(): complete = jnp.concatenate(lax.all_gather(weight, 'batch'), axis=2)  31.3 us
    all_gather x4, waiting for transfers between devices, convolve(): complete = jnp.concatenate(lax.all_gather(weight, 'batch'), axis=2)  23.1 us
    dot_general x13, matrix products, apply_taps(): jnp.einsum('bhwk,kc->bhwc', stacked, weight_piece[row_tap], preferred_ele...  14.4 us
    slice x4, local copies, waits for them, and re-layouts, apply_taps(): weight_piece[row_tap]  9.91 us
    ppermute x4, starting transfers between devices, extended(): lax.ppermute(lax.slice_in_dim(block, block.shape[dim] - width, None, axis...  7.96 us
    ppermute x4, starting transfers between devices, extended(): lax.ppermute(lax.slice_in_dim(block, 0, width, axis=dim), axis, backward)  5.35 us
    unnamed x38, local copies, waits for them, and re-layouts  4.7 us
  transfers between devices with their start and end apart: 12, of which 3 were waited for; matrix products, arithmetic and copies ran while one was open for 14% of the time, Pallas kernels for 0%

profile of v1, /device:TPU:0, one launch (start us, length us, event | category | flops | bytes accessed | tf_op | source)
XLA Modules:
  0.0 171.1 jit_solution(10728988175701597753)
XLA Ops:
  6.5 2.4 %fusion.155 = (bf16[1,1,3,960,40]{3,4,2,1,0:T(8,128)(2,1)}, bf16[1,1,3,960,40]{3,4,2,1,0:T(8,128)(2,1)}, bf16[1,1,3,960,40]{3,4,2,1,0:T(8,128)(2,1)}, bf16[1,1,3,960,40]{3,4,2,1,0:T(8,128)(2,1)}) fusion(bf16[2,2,3,960,40]{3,4,2,1,0:T(8,128)(2,1)} %param.10), kind=kLoop, calls=%fused_computation.205 | loop fusion | bytes 1843200 | tf_op jit(solution)/shard_map/slice | solution.py:80
  9.0 0.7 all-gather.11.cloned.1.call-update
  9.8 0.7 all-gather.13.cloned.1.call-update
  10.5 0.2 convert_reduce_fusion.1
  10.9 0.1 reduce_sum.97
  11.0 0.1 reduce_sum.100
  11.1 11.4 %all-reduce.7 = (f32[1,1,1,32,1]{3,4,2,1,0:T(1,128)S(1)}, f32[1,1,1,32,1]{3,4,2,1,0:T(1,128)S(1)}) all-reduce(f32[1,1,1,32,1]{3,4,2,1,0:T(1,128)S(1)} %bitcast.204, f32[1,1,1,32,1]{3,4,2,1,0:T(1,128)S(1)} %bitcast.202), channel_id=1, replica_groups=mesh['rows'=4,'batch'=8] {'rows'}, use_global_device_ids=true, to_apply=%region_5.6 | all-reduce | flops 64 | bytes 512 | tf_op jit(solution)/shard_map/psum | solution.py:29
  23.0 0.3 fusion.116
  23.3 1.5 collective-permute-start
  24.9 1.3 collective-permute-start.1
  26.2 16.7 %all_gather.23 = bf16[8,1,320,40]{2,3,1,0:T(8,128)(2,1)} all-gather(bf16[1,1,320,40]{2,3,1,0:T(8,128)(2,1)S(1)} %get-tuple-element.78), channel_id=1, replica_groups=mesh['rows'=4,'batch'=8] {'batch'}, dimensions={0}, use_global_device_ids=true | all-gather | bytes 230400 | tf_op jit(solution)/shard_map/all_gather | solution.py:71
  42.9 14.7 %all_gather.20 = bf16[8,1,320,40]{2,3,1,0:T(8,128)(2,1)S(1)} all-gather(bf16[1,1,320,40]{2,3,1,0:T(8,128)(2,1)S(1)} %get-tuple-element.77), channel_id=1, replica_groups=mesh['rows'=4,'batch'=8] {'batch'}, dimensions={0}, use_global_device_ids=true | all-gather | bytes 230400 | tf_op jit(solution)/shard_map/all_gather | solution.py:71
  57.6 0.2 fusion.134
  57.8 1.0 fusion.159
  58.8 1.7 %fusion.154 = (bf16[1,960,8,40]{1,3,0,2:T(8,128)(2,1)S(1)}, bf16[1,960,8,40]{1,3,0,2:T(8,128)(2,1)S(1)}, bf16[1,960,8,40]{1,3,0,2:T(8,128)(2,1)S(1)}) fusion(bf16[3,960,8,40]{1,3,0,2:T(8,128)(2,1)} %bitcast.184), kind=kLoop, calls=%fused_computation.204 | loop fusion | bytes 3686400 | tf_op jit(solution)/shard_map/slice | solution.py:60
  60.5 0.8 fusion.53
  61.3 0.8 convolution_add_fusion.9
  62.2 0.8 convert_reduce_fusion.3
  63.4 11.2 %all-reduce.6 = (f32[1,1,1,32,1]{3,4,2,1,0:T(1,128)S(1)}, f32[1,1,1,32,1]{3,4,2,1,0:T(1,128)S(1)}) all-reduce(f32[1,1,1,32,1]{3,4,2,1,0:T(1,128)S(1)} %bitcast.205, f32[1,1,1,32,1]{3,4,2,1,0:T(1,128)S(1)} %bitcast.200), channel_id=1, replica_groups=mesh['rows'=4,'batch'=8] {'rows'}, use_global_device_ids=true, to_apply=%region_11.12 | all-reduce | flops 64 | bytes 512 | tf_op jit(solution)/shard_map/psum | solution.py:29
  75.0 0.3 fusion.136
  75.3 3.3 %collective-permute-start.2 = (bf16[1,1,96,320]{3,2,1,0:T(8,128)(2,1)S(1)}, bf16[1,1,96,320]{3,2,1,0:T(8,128)(2,1)S(1)}, u32[]{:S(2)}, u32[]{:S(2)}) collective-permute-start(bf16[1,1,96,320]{3,2,1,0:T(8,128)(2,1)S(1)} %get-tuple-element.74), channel_id=1, source_target_pairs={{0,8},{8,16},{16,24},{1,9},{9,17},{17,25},{2,10},{10,18},{18,26},{... | collective-permute-start | bytes 184328 | tf_op jit(solution)/shard_map/ppermute | solution.py:15
  78.6 1.3 collective-permute-start.3
  80.0 2.9 %fusion.153 = (bf16[1,960,8,40]{1,3,0,2:T(8,128)(2,1)S(1)}, bf16[1,960,8,40]{1,3,0,2:T(8,128)(2,1)}, bf16[1,960,8,40]{1,3,0,2:T(8,128)(2,1)}) fusion(bf16[3,960,8,40]{1,3,0,2:T(8,128)(2,1)} %bitcast.182), kind=kLoop, calls=%fused_computation.203 | loop fusion | bytes 3686400 | tf_op jit(solution)/shard_map/slice | solution.py:60
  82.9 18.0 %all-gather.13.cloned.1.call-done = bf16[8,1,3,960,40]{3,4,2,1,0:T(8,128)(2,1)} async-done(((bf16[1,1,3,960,40]{3,4,2,1,0:T(8,128)(2,1)}), bf16[8,1,3,960,40]{3,4,2,1,0:T(8,128)(2,1)}) %all-gather.13.cloned.1.call-update) | async-done | bytes 1843216 | tf_op jit(solution)/shard_map/all_gather | solution.py:71
  100.8 2.5 %fusion.152 = (bf16[1,960,8,40]{1,3,0,2:T(8,128)(2,1)S(1)}, bf16[1,960,8,40]{1,3,0,2:T(8,128)(2,1)S(1)}, bf16[1,960,8,40]{1,3,0,2:T(8,128)(2,1)}) fusion(bf16[3,960,8,40]{1,3,0,2:T(8,128)(2,1)} %bitcast.183), kind=kLoop, calls=%fused_computation.202 | loop fusion | bytes 3686400 | tf_op jit(solution)/shard_map/slice | solution.py:60
  103.4 0.6 copy-done.12
  104.0 0.6 copy-done.8
  104.6 0.2 select_maximum_fusion.4
  104.8 0.3 fusion.158
  105.2 0.7 copy-done.5
  105.9 0.8 fusion.42
  106.7 0.3 copy-done.4
  107.0 0.8 convolution_add_fusion.7
  107.9 1.5 convert_reduce_fusion
  109.3 0.8 reduce_sum.114
  110.1 0.1 reduce_sum.115
  110.3 0.8 reduce_sum.144
  111.2 9.8 %all-reduce.5 = (f32[1,1,1,32,1]{3,4,2,1,0:T(1,128)S(1)}, f32[1,1,1,32,1]{3,4,2,1,0:T(1,128)S(1)}) all-reduce(f32[1,1,1,32,1]{3,4,2,1,0:T(1,128)S(1)} %bitcast.206, f32[1,1,1,32,1]{3,4,2,1,0:T(1,128)S(1)} %bitcast.201), channel_id=1, replica_groups=mesh['rows'=4,'batch'=8] {'rows'}, use_global_device_ids=true, to_apply=%region_17.18 | all-reduce | flops 64 | bytes 512 | tf_op jit(solution)/shard_map/psum | solution.py:29
  121.4 0.3 fusion.126
  121.7 1.6 collective-permute-start.4
  123.3 1.5 collective-permute-start.5
  124.8 5.1 %all-gather.15.cloned.1.call-done = bf16[8,1,3,960,40]{3,4,2,1,0:T(8,128)(2,1)} async-done(((bf16[1,1,3,960,40]{3,4,2,1,0:T(8,128)(2,1)}), bf16[8,1,3,960,40]{3,4,2,1,0:T(8,128)(2,1)}) %all-gather.15.cloned.1.call-update) | async-done | bytes 1843216 | tf_op jit(solution)/shard_map/all_gather | solution.py:71
  129.9 2.7 %fusion.151 = (bf16[1,960,8,40]{1,3,0,2:T(8,128)(2,1)S(1)}, bf16[1,960,8,40]{1,3,0,2:T(8,128)(2,1)}, bf16[1,960,8,40]{1,3,0,2:T(8,128)(2,1)}) fusion(bf16[3,960,8,40]{1,3,0,2:T(8,128)(2,1)} %bitcast.181), kind=kLoop, calls=%fused_computation.201 | loop fusion | bytes 3686400 | tf_op jit(solution)/shard_map/slice | solution.py:60
  132.6 0.6 copy-done.14
  133.2 0.6 copy-done.10
  133.9 0.2 select_maximum_fusion.2
  134.1 0.3 fusion.157
  134.4 0.7 copy-done.1
  135.2 0.8 fusion.31
  136.0 0.8 convolution_add_fusion.5
  136.8 0.8 convert_reduce_fusion.2
  138.1 9.8 %all-reduce.4 = (f32[1,1,1,32,1]{3,4,2,1,0:T(1,128)S(1)}, f32[1,1,1,32,1]{3,4,2,1,0:T(1,128)S(1)}) all-reduce(f32[1,1,1,32,1]{3,4,2,1,0:T(1,128)S(1)} %bitcast.203, f32[1,1,1,32,1]{3,4,2,1,0:T(1,128)S(1)} %bitcast.199), channel_id=1, replica_groups=mesh['rows'=4,'batch'=8] {'rows'}, use_global_device_ids=true, to_apply=%region_23.24 | all-reduce | flops 64 | bytes 512 | tf_op jit(solution)/shard_map/psum | solution.py:29
  148.3 0.3 fusion.135
  148.7 1.6 collective-permute-start.6
  150.3 1.3 collective-permute-start.7
  151.6 1.4 fusion.10
  153.0 3.8 %collective-permute-done.7 = bf16[1,1,96,320]{3,2,1,0:T(8,128)(2,1)S(1)} collective-permute-done((bf16[1,1,96,320]{3,2,1,0:T(8,128)(2,1)S(1)}, bf16[1,1,96,320]{3,2,1,0:T(8,128)(2,1)S(1)}, u32[]{:S(2)}, u32[]{:S(2)}) %collective-permute-start.7) | collective-permute-done | bytes 61472 | tf_op jit(solution)/shard_map/ppermute | solution.py:18
  156.9 0.2 select_maximum_fusion
  157.1 1.1 fusion.156
  158.2 0.8 fusion.20
  159.0 0.3 copy-done.2
  159.3 1.7 %convolution_add_fusion.3 = f32[6,96,320]{2,1,0:T(8,128)} fusion(f32[6,96,320]{2,1,0:T(8,128)S(1)} %fusion.20, bf16[960,320,1]{0,1,2:T(8,128)(2,1)S(1)} %bitcast.190, bf16[1,6,96,320]{3,2,1,0:T(8,128)(2,1)S(1)} %get-tuple-element.46, bf16[1,6,96,320]{3,2,1,0:T(8,128)(2,1)S(1)} %fusion.135, bf16[1,6,96,320]{3,2,1,0:T(8,128)(2,1)S(1)} %get-tuple-element.47), kind=kOutput, calls=%fused_computation.20 | convolution fusion | flops 357396480 | bytes 3194880 | tf_op jit(solution)/shard_map/bhwk,kc->bhwc/dot_general | solution.py:59
  161.0 2.5 %fusion.9 = bf16[1,1,6,96,320]{4,3,2,1,0:T(8,128)(2,1)S(1)} fusion(bf16[320,320,1]{0,1,2:T(8,128)(2,1)S(1)} %bitcast.198, f32[6,96,320]{2,1,0:T(8,128)} %convolution_add_fusion.3, bf16[960,320,1]{0,1,2:T(8,128)(2,1)S(1)} %bitcast.187, bf16[1,6,96,320]{3,2,1,0:T(8,128)(2,1)S(1)} %get-tuple-element.88, ...), kind=kOutput, calls=%fused_computation.35 | convolution fusion | flops 477573120 | bytes 3829760 | tf_op jit(solution)/shard_map/bhwk,kc->bhwc/dot_general | solution.py:59
  163.5 1.1 pad_maximum_fusion.8
  (82 shorter events, 3.2 us)
Async XLA Ops:
  6.5 4.0 %copy-start = (bf16[1,6,96,320]{3,2,1,0:T(8,128)(2,1)S(1)}, bf16[1,6,96,320]{3,2,1,0:T(8,128)(2,1)}, u32[]{:S(2)}) copy-start(bf16[1,6,96,320]{3,2,1,0:T(8,128)(2,1)} %param.6) | copy-start | bytes 1105924
  6.5 16.4 %copy-start.18 = (f32[2,2,320]{2,1,0:T(2,128)S(1)}, f32[2,2,320]{2,1,0:T(2,128)}, u32[]{:S(2)}) copy-start(f32[2,2,320]{2,1,0:T(2,128)} %param.8) | copy-start | bytes 15364
  6.5 16.4 %copy-start.17 = (f32[2,2,320]{2,1,0:T(2,128)S(1)}, f32[2,2,320]{2,1,0:T(2,128)}, u32[]{:S(2)}) copy-start(f32[2,2,320]{2,1,0:T(2,128)} %param.9) | copy-start | bytes 15364
  6.5 52.2 %all-gather.9.cloned.1.call-start = ((), (), s32[]{:S(2)}) async-start(), calls=%async_computation | async-start | bytes 2211840 | tf_op jit(solution)/shard_map/all_gather | solution.py:71
  9.0 71.0 %all-gather.11.cloned.1.call-start = ((), (), s32[]{:S(2)}) async-start(), calls=%async_computation.1 | async-start | bytes 2211840 | tf_op jit(solution)/shard_map/all_gather | solution.py:71
  9.0 17.2 %copy-start.16 = (bf16[2,1,320,40]{2,3,1,0:T(8,128)(2,1)S(1)}, bf16[2,1,320,40]{2,3,1,0:T(8,128)(2,1)}, u32[]{:S(2)}) copy-start(bf16[2,1,320,40]{2,3,1,0:T(8,128)(2,1)} %param.11) | copy-start | bytes 153604
  9.7 91.1 %all-gather.13.cloned.1.call-start = ((), (), s32[]{:S(2)}) async-start(), calls=%async_computation.2 | async-start | bytes 2211840 | tf_op jit(solution)/shard_map/all_gather | solution.py:71
  10.5 119.4 %all-gather.15.cloned.1.call-start = ((), (), s32[]{:S(2)}) async-start(), calls=%async_computation.3 | async-start | bytes 2211840 | tf_op jit(solution)/shard_map/all_gather | solution.py:71
  23.3 34.2 %collective-permute-start = (bf16[1,1,96,320]{3,2,1,0:T(8,128)(2,1)S(1)}, bf16[1,1,96,320]{3,2,1,0:T(8,128)(2,1)S(1)}, u32[]{:S(2)}, u32[]{:S(2)}) collective-permute-start(bf16[1,1,96,320]{3,2,1,0:T(8,128)(2,1)S(1)} %get-tuple-element.76), channel_id=1, source_target_pairs={{0,8},{8,16},{16,24},{1,9},{9,17},{17,25},{2,10},{10,18},{18,26},{... | collective-permute-start | bytes 184328 | tf_op jit(solution)/shard_map/ppermute | solution.py:15
  24.9 32.7 %collective-permute-start.1 = (bf16[1,1,96,320]{3,2,1,0:T(8,128)(2,1)S(1)}, bf16[1,1,96,320]{3,2,1,0:T(8,128)(2,1)S(1)}, u32[]{:S(2)}, u32[]{:S(2)}) collective-permute-start(bf16[1,1,96,320]{3,2,1,0:T(8,128)(2,1)S(1)} %get-tuple-element.75), channel_id=1, source_target_pairs={{8,0},{16,8},{24,16},{9,1},{17,9},{25,17},{10,2},{18,10},{26,18},{... | collective-permute-start | bytes 184328 | tf_op jit(solution)/shard_map/ppermute | solution.py:18
  58.8 1.8 %copy-start.6 = (bf16[1,6,96,320]{3,2,1,0:T(8,128)(2,1)S(1)}, bf16[1,6,96,320]{3,2,1,0:T(8,128)(2,1)}, u32[]{:S(2)}) copy-start(bf16[1,6,96,320]{3,2,1,0:T(8,128)(2,1)} %get-tuple-element.67) | copy-start | bytes 1105924
  75.3 28.0 %collective-permute-start.2 = (bf16[1,1,96,320]{3,2,1,0:T(8,128)(2,1)S(1)}, bf16[1,1,96,320]{3,2,1,0:T(8,128)(2,1)S(1)}, u32[]{:S(2)}, u32[]{:S(2)}) collective-permute-start(bf16[1,1,96,320]{3,2,1,0:T(8,128)(2,1)S(1)} %get-tuple-element.74), channel_id=1, source_target_pairs={{0,8},{8,16},{16,24},{1,9},{9,17},{17,25},{2,10},{10,18},{18,26},{... | collective-permute-start | bytes 184328 | tf_op jit(solution)/shard_map/ppermute | solution.py:15
  78.6 24.7 %collective-permute-start.3 = (bf16[1,1,96,320]{3,2,1,0:T(8,128)(2,1)S(1)}, bf16[1,1,96,320]{3,2,1,0:T(8,128)(2,1)S(1)}, u32[]{:S(2)}, u32[]{:S(2)}) collective-permute-start(bf16[1,1,96,320]{3,2,1,0:T(8,128)(2,1)S(1)} %get-tuple-element.73), channel_id=1, source_target_pairs={{8,0},{16,8},{24,16},{9,1},{17,9},{25,17},{10,2},{18,10},{26,18},{... | collective-permute-start | bytes 184328 | tf_op jit(solution)/shard_map/ppermute | solution.py:18
  103.4 0.6 copy-start.12
  104.0 0.6 copy-start.8
  104.8 1.1 copy-start.5
  104.8 1.1 copy-start.13
  105.9 1.1 copy-start.4
  107.0 0.9 copy-start.9
  121.7 10.9 %collective-permute-start.4 = (bf16[1,1,96,320]{3,2,1,0:T(8,128)(2,1)S(1)}, bf16[1,1,96,320]{3,2,1,0:T(8,128)(2,1)S(1)}, u32[]{:S(2)}, u32[]{:S(2)}) collective-permute-start(bf16[1,1,96,320]{3,2,1,0:T(8,128)(2,1)S(1)} %get-tuple-element.72), channel_id=1, source_target_pairs={{0,8},{8,16},{16,24},{1,9},{9,17},{17,25},{2,10},{10,18},{18,26},{... | collective-permute-start | bytes 184328 | tf_op jit(solution)/shard_map/ppermute | solution.py:15
  123.3 9.3 %collective-permute-start.5 = (bf16[1,1,96,320]{3,2,1,0:T(8,128)(2,1)S(1)}, bf16[1,1,96,320]{3,2,1,0:T(8,128)(2,1)S(1)}, u32[]{:S(2)}, u32[]{:S(2)}) collective-permute-start(bf16[1,1,96,320]{3,2,1,0:T(8,128)(2,1)S(1)} %get-tuple-element.71), channel_id=1, source_target_pairs={{8,0},{16,8},{24,16},{9,1},{17,9},{25,17},{10,2},{18,10},{26,18},{... | collective-permute-start | bytes 184328 | tf_op jit(solution)/shard_map/ppermute | solution.py:18
  132.6 0.6 copy-start.14
  133.2 0.6 copy-start.10
  134.1 1.1 copy-start.1
  134.1 1.1 copy-start.15
  136.0 0.9 copy-start.11
  148.7 4.3 %collective-permute-start.6 = (bf16[1,1,96,320]{3,2,1,0:T(8,128)(2,1)S(1)}, bf16[1,1,96,320]{3,2,1,0:T(8,128)(2,1)S(1)}, u32[]{:S(2)}, u32[]{:S(2)}) collective-permute-start(bf16[1,1,96,320]{3,2,1,0:T(8,128)(2,1)S(1)} %get-tuple-element.70), channel_id=1, source_target_pairs={{0,8},{8,16},{16,24},{1,9},{9,17},{17,25},{2,10},{10,18},{18,26},{... | collective-permute-start | bytes 184328 | tf_op jit(solution)/shard_map/ppermute | solution.py:15
  150.3 6.6 %collective-permute-start.7 = (bf16[1,1,96,320]{3,2,1,0:T(8,128)(2,1)S(1)}, bf16[1,1,96,320]{3,2,1,0:T(8,128)(2,1)S(1)}, u32[]{:S(2)}, u32[]{:S(2)}) collective-permute-start(bf16[1,1,96,320]{3,2,1,0:T(8,128)(2,1)S(1)} %get-tuple-element.69), channel_id=1, source_target_pairs={{8,0},{16,8},{24,16},{9,1},{17,9},{25,17},{10,2},{18,10},{26,18},{... | collective-permute-start | bytes 184328 | tf_op jit(solution)/shard_map/ppermute | solution.py:18
  157.1 1.1 copy-start.3
  158.2 1.1 copy-start.2
  159.3 1.7 %copy-start.7 = (bf16[8,1,320,40]{2,3,1,0:T(8,128)(2,1)S(1)}, bf16[8,1,320,40]{2,3,1,0:T(8,128)(2,1)}, u32[]{:S(2)}) copy-start(bf16[8,1,320,40]{2,3,1,0:T(8,128)(2,1)} %all_gather.23) | copy-start | bytes 614404
Sparse Core Ops, SparseCore 0:
  9.1 32.4 all-gather.8
  43.2 28.4 all-gather.10
  73.3 27.4 all-gather.12
  102.3 27.4 all-gather.14
